TPU v7x, 512 devices: a whole 4x4x16 slice. The times are simulated.
512 devices in a mesh: ep: 64 (over x, z), tp: 8 (over y, core).
Axes of the slice: x: 4, y: 4, z: 16, core: 2. Of those that a mesh axis runs over, the one named last changes fastest.
Arguments:
- tokens: bfloat16 [1024, 4096], P('ep', 'tp'), may hold values from -6 to 6
- expert_ids: int32 [1024, 8], P('ep'), may hold values from 0 to 63, as said below
- route_weight: float32 [1024, 8], P('ep'), may hold values from 0.05 to 0.6
- gate_weight: bfloat16 [64, 1536, 4096], P('ep', 'tp'), may hold values from -0.09375 to 0.09375
- up_weight: bfloat16 [64, 1536, 4096], P('ep', 'tp'), may hold values from -0.09375 to 0.09375
- down_weight: bfloat16 [64, 1536, 4096], P('ep', 'tp'), may hold values from -0.21875 to 0.21875
Outputs:
- moe_out: bfloat16 [1024, 4096], P('ep', 'tp')
- act_absmax: float32 [2, 64], P(None, 'ep')
Inputs may be any that keep to these rules, and one draw needn't show every extreme that they name: `expert_ids`: each row names 8 different experts. Exactly 2 experts are named more than 2 times among the rows of one index of ep, in every such block, and at most 8 times; one of them is named exactly 8 times in every block, the other reaches 8 in some block. Every other expert is named at most 2 times among the rows of one index of ep, and one of them exactly 2 times in every block.
All inputs are finite; a program needn't handle non-finite values.
Results may differ from a plain program's by a relative error of at most 0.015.
Values may be sent and summed in bfloat16 or wider, within the bound.
No kernel may reach another device: no remote copies, remote signals or barrier semaphores. Data moves between devices by JAX's collectives and lax.ppermute only.
A program may use at most 64 MiB of HBM per device.

v0:
```python
import jax
import jax.numpy as jnp
from jax import lax
from jax.sharding import PartitionSpec as P

TOP = 8
EXP_DEV = 1


def copy_for_each(array, axis):
    count = lax.axis_size(axis)
    return lax.all_to_all(
        jnp.broadcast_to(array[None], (count, *array.shape)), axis, 0, 0, tiled=True
    )


def taken_together(array, axis):
    return copy_for_each(array, axis).max(axis=0)


def group_ranks(group_ids, group_total):
    onehot = (group_ids[:, None] == jnp.arange(group_total, dtype=jnp.int32)[None, :]).astype(
        jnp.int32
    )
    return jnp.sum((jnp.cumsum(onehot, axis=0) - 1) * onehot, axis=1)


def place_slots(slot_ids, valid, owner_row, slot_total):
    target = jnp.where(valid, slot_ids, slot_total)
    source = jnp.zeros((slot_total,), jnp.int32).at[target].set(owner_row, mode="drop")
    filled = jnp.zeros((slot_total,), jnp.bool_).at[target].set(True, mode="drop")
    return (source, filled)


def project_rows(row_block, weight):
    return lax.dot_general(
        row_block, weight, (((1,), (1,)), ((), ())), preferred_element_type=jnp.float32
    )


def serve_rows(row_block, gate_weight, up_weight, down_weight):
    senders, slot_count, feat_width = row_block.shape
    flat_rows = row_block.reshape(senders * slot_count, feat_width)
    gate_val = project_rows(flat_rows, gate_weight[0])
    up_val = project_rows(flat_rows, up_weight[0])
    hidden = (jax.nn.silu(gate_val) * up_val).astype(jnp.bfloat16)
    partial_value = jnp.dot(hidden, down_weight[0], preferred_element_type=jnp.float32)
    summed = lax.psum_scatter(
        partial_value.reshape(senders, slot_count, feat_width).astype(jnp.bfloat16),
        "tp",
        scatter_dimension=2,
        tiled=True,
    )
    returned_rows = lax.all_to_all(summed, "ep", split_axis=0, concat_axis=0, tiled=True)
    input_peak = (
        jnp.max(jnp.abs(flat_rows), axis=1).astype(jnp.float32).reshape(senders, slot_count)
    )
    hidden_peak = jnp.max(jnp.abs(hidden), axis=1).astype(jnp.float32).reshape(senders, slot_count)
    return (returned_rows, input_peak, hidden_peak)


def body(tokens, expert_ids, route_weight, gate_weight, up_weight, down_weight):
    senders = lax.axis_size("ep")
    experts = senders * EXP_DEV
    tok_rows = tokens.shape[0]
    common = tok_rows * TOP // experts
    hot_most = min(tok_rows, 4 * common)
    pick_ids = expert_ids.reshape(-1)
    owner_row = jnp.arange(pick_ids.shape[0], dtype=jnp.int32) // TOP
    zero_row = jnp.zeros((), jnp.bfloat16)
    rank_of = group_ranks(pick_ids, experts)
    send_slot = pick_ids * hot_most + rank_of
    source, filled = place_slots(
        send_slot, jnp.ones(pick_ids.shape, jnp.bool_), owner_row, experts * hot_most
    )
    outgoing = jnp.where(filled[:, None], tokens[source], zero_row).reshape(
        experts, hot_most, tokens.shape[1]
    )
    returned_rows, input_peak, hidden_peak = serve_rows(
        lax.all_gather(
            lax.all_to_all(outgoing, "ep", split_axis=0, concat_axis=0, tiled=True),
            "tp",
            axis=2,
            tiled=True,
        ),
        gate_weight,
        up_weight,
        down_weight,
    )
    out_table = returned_rows.reshape(experts * hot_most, returned_rows.shape[2])
    top_hidden = taken_together(jnp.max(hidden_peak), "tp")
    column = jnp.stack([jnp.max(input_peak), top_hidden])
    picked = out_table[send_slot].astype(jnp.float32).reshape(tok_rows, TOP, out_table.shape[1])
    moe_out = jnp.sum(picked * route_weight[:, :, None], axis=1).astype(jnp.bfloat16)
    act_absmax = column.reshape(2, 1)
    return (moe_out, act_absmax)


def solution(mesh):
    return jax.shard_map(
        body,
        mesh=mesh,
        in_specs=(
            P("ep", "tp"),
            P("ep", None),
            P("ep", None),
            P("ep", "tp", None),
            P("ep", "tp", None),
            P("ep", "tp", None),
        ),
        out_specs=(P("ep", "tp"), P(None, "ep")),
        check_vma=False,
    )
```

profile of v0, /device:TPU:31, one launch (start us, length us, event | category | flops | bytes accessed | tf_op | source)
XLA Modules:
  0.0 207.1 jit_solution(10847064991824207916)
XLA Ops:
  7.2 0.0 all-gather.2.cloned.1.call-start
  7.2 0.9 copy.21
  8.1 0.7 broadcast_multiply_fusion
  8.8 0.1 eq.15
  8.9 0.1 fusion.19
  9.0 0.2 reduce_window_sum.11
  9.1 0.2 select_reduce_fusion
  9.3 0.1 copy.20
  9.4 0.1 mul.37
  9.5 1.0 scatter_custom_fusion.1
  10.5 1.0 scatter_custom_fusion
  11.5 0.1 broadcast_in_dim.38
  11.6 2.7 %gather_fusion = bf16[512,512]{1,0:T(8,128)(2,1)S(1)} fusion(bf16[16,512]{1,0:T(8,128)(2,1)} %param.6, s32[1024]{0:T(1024)S(1)} %pad_clamp_fusion.1), kind=kCustom, calls=%fused_computation | custom fusion | bytes 1050624 | tf_op jit(solution)/shard_map/gather | solution.py:76
  14.3 0.1 bitcast_select_fusion
  14.5 47.8 %all_to_all.16 = bf16[64,8,512]{2,1,0:T(8,128)(2,1)} all-to-all(bf16[64,8,512]{2,1,0:T(8,128)(2,1)S(1)} %bitcast_select_fusion), channel_id=1, replica_groups=mesh['ep'=64,'tp'=8] {'ep'}, dimensions={0} | all-to-all | bytes 1048576 | tf_op jit(solution)/shard_map/all_to_all | solution.py:81
  62.3 0.0 reduce-scatter.2.cloned.1.call-start
  62.4 33.3 %all-gather.2.cloned.1.call-done = bf16[64,8,4096]{2,1,0:T(8,128)(2,1)} async-done(((bf16[64,8,512]{2,1,0:T(8,128)(2,1)}), bf16[64,8,4096]{2,1,0:T(8,128)(2,1)}) %all-gather.2.cloned.1.call-update) | async-done | bytes 4194320 | tf_op jit(solution)/shard_map/all_gather | solution.py:80
  95.7 4.3 %fusion.2 = f32[512,192]{0,1:T(8,128)S(1)} fusion(bf16[64,8,4096]{2,1,0:T(8,128)(2,1)} %all-gather.2.cloned.1.call-done, bf16[1,192,4096]{2,1,0:T(8,128)(2,1)} %param.9), kind=kOutput, calls=%fused_computation.7 | convolution fusion | flops 805306368 | bytes 6160384 | tf_op jit(solution)/shard_map/dot_general | solution.py:36
  100.0 2.3 %abs_reduce_fusion.1 = (bf16[]{:T(256)}, bf16[512,192]{0,1:T(8,128)(2,1)S(1)}) fusion(bf16[1,192,4096]{2,1,0:T(8,128)(2,1)S(1)} %copy-done.3, bf16[64,8,4096]{2,1,0:T(8,128)(2,1)S(1)} %copy-done.1, f32[512,192]{0,1:T(8,128)S(1)} %fusion.2), kind=kOutput, calls=%fused_computation.19 | convolution fusion | flops 806092800 | bytes 6356994 | tf_op jit(solution)/shard_map/dot_general | solution.py:36
  102.3 0.1 copy.22
  102.4 3.2 %convolution_convert_fusion = bf16[64,8,4096]{2,1,0:T(8,128)(2,1)} fusion(bf16[1,192,4096]{2,1,0:T(8,128)(2,1)S(1)} %copy-done, bf16[512,192]{1,0:T(8,128)(2,1)S(1)} %copy.22), kind=kOutput, calls=%fused_computation.4 | convolution fusion | flops 807403520 | bytes 5963776 | tf_op jit(solution)/shard_map/dot_general | solution.py:47
  105.7 0.7 broadcast_in_dim.42
  106.3 8.0 %all_to_all.17 = f32[8,1,1]{2,1,0:T(1,128)S(1)} all-to-all(f32[8,1,1]{2,1,0:T(1,128)S(1)} %broadcast_in_dim.42), channel_id=1, replica_groups=mesh['ep'=64,'tp'=8] {'tp'}, dimensions={0} | all-to-all | bytes 64 | tf_op jit(solution)/shard_map/all_to_all | solution.py:12
  114.3 37.1 %reduce-scatter.2.cloned.1.call-done = bf16[64,8,512]{2,1,0:T(8,128)(2,1)} async-done(((bf16[64,8,4096]{2,1,0:T(8,128)(2,1)}), bf16[64,8,512]{2,1,0:T(8,128)(2,1)}) %reduce-scatter.2.cloned.1.call-update) | async-done | bytes 524304 | tf_op jit(solution)/shard_map/reduce_scatter | solution.py:48
  151.4 15.3 %all-to-all-start.1 = ((bf16[64,8,512]{2,1,0:T(8,128)(2,1)}), bf16[64,8,512]{2,1,0:T(8,128)(2,1)S(1)}, u32[]{:S(2)}, u32[]{:S(2)}) async-start(bf16[64,8,512]{2,1,0:T(8,128)(2,1)} %reduce-scatter.2.cloned.1.call-done), calls=%async_computation.2 | async-start | bytes 1048576 | tf_op jit(solution)/shard_map/all_to_all | solution.py:54
  166.8 0.1 copy.23
  166.9 3.4 %abs_reduce_fusion = bf16[]{:T(256)} fusion(bf16[64,8,4096]{2,1,0:T(8,128)(2,1)} %all-gather.2.cloned.1.call-done), kind=kLoop, calls=%fused_computation.9 | loop fusion | flops 4194303 | bytes 4194306 | tf_op jit(solution)/shard_map/reduce_max | solution.py:92
  170.9 0.6 reduce_max.46
  171.5 1.2 maximum_bitcast_fusion
  172.8 25.9 %all-to-all-done.1 = bf16[64,8,512]{2,1,0:T(8,128)(2,1)S(1)} async-done(((bf16[64,8,512]{2,1,0:T(8,128)(2,1)}), bf16[64,8,512]{2,1,0:T(8,128)(2,1)S(1)}, u32[]{:S(2)}, u32[]{:S(2)}) %all-to-all-start.1) | async-done | bytes 524320 | tf_op jit(solution)/shard_map/all_to_all | solution.py:54
  198.7 0.8 gather_fusion.1
  199.5 0.8 fusion.17
  (16 shorter events, 0.1 us)
Async XLA Ops:
  7.2 95.3 %copy-start = (bf16[1,192,4096]{2,1,0:T(8,128)(2,1)S(1)}, bf16[1,192,4096]{2,1,0:T(8,128)(2,1)}, u32[]{:S(2)}) copy-start(bf16[1,192,4096]{2,1,0:T(8,128)(2,1)} %param.11) | copy-start | bytes 4718596
  7.2 88.5 %all-gather.2.cloned.1.call-start = ((), (), s32[]{:S(2)}) async-start(), calls=%async_computation.4 | async-start | bytes 4718592 | tf_op jit(solution)/shard_map/all_gather | solution.py:80
  14.5 85.5 %copy-start.3 = (bf16[1,192,4096]{2,1,0:T(8,128)(2,1)S(1)}, bf16[1,192,4096]{2,1,0:T(8,128)(2,1)}, u32[]{:S(2)}) copy-start(bf16[1,192,4096]{2,1,0:T(8,128)(2,1)} %param.10) | copy-start | bytes 4718596
  62.3 89.1 %reduce-scatter.2.cloned.1.call-start = ((), (), s32[]{:S(2)}) async-start(), calls=%async_computation.5 | async-start | bytes 4718592 | tf_op jit(solution)/shard_map/reduce_scatter | solution.py:48
  95.7 4.4 %copy-start.1 = (bf16[64,8,4096]{2,1,0:T(8,128)(2,1)S(1)}, bf16[64,8,4096]{2,1,0:T(8,128)(2,1)}, u32[]{:S(2)}) copy-start(bf16[64,8,4096]{2,1,0:T(8,128)(2,1)} %all-gather.2.cloned.1.call-done) | copy-start | bytes 12582916
  102.4 64.4 %copy-start.2 = (f32[16,8]{0,1:T(8,128)S(1)}, f32[16,8]{0,1:T(8,128)}, u32[]{:S(2)}) copy-start(f32[16,8]{0,1:T(8,128)} %param.8) | copy-start | bytes 1540
  151.4 47.3 %all-to-all-start.1 = ((bf16[64,8,512]{2,1,0:T(8,128)(2,1)}), bf16[64,8,512]{2,1,0:T(8,128)(2,1)S(1)}, u32[]{:S(2)}, u32[]{:S(2)}) async-start(bf16[64,8,512]{2,1,0:T(8,128)(2,1)} %reduce-scatter.2.cloned.1.call-done), calls=%async_computation.2 | async-start | bytes 1048576 | tf_op jit(solution)/shard_map/all_to_all | solution.py:54
Sparse Core Ops, SparseCore 0:
  62.4 33.1 all-gather.1
  105.8 45.5 reduce-scatter.1
where the time goes:
time: 208 us; the launch traced here: 207 us
  waiting for transfers between devices  96.4 us (46%)
  blocking collectives  55.8 us (27%)
  starting transfers between devices  15.4 us (7%)
  between operations  14.9 us (7%)
  matrix products  9.82 us (5%)
  local copies, waits for them, and re-layouts  7.63 us (4%)
  other arithmetic  7.25 us (3%)
    all_to_all x1, blocking collectives, body(): lax.all_to_all(outgoing, 'ep', split_axis=0, concat_axis=0, tiled=True)  47.8 us
    reduce_scatter x1, waiting for transfers between devices, serve_rows(): lax.psum_scatter(partial_value.reshape(senders, slot_count, feat_width).a...  37.1 us
    all_gather x1, waiting for transfers between devices, body(): lax.all_gather(lax.all_to_all(outgoing, 'ep', split_axis=0, concat_axis=0...  33.3 us
    all_to_all x1, waiting for transfers between devices, serve_rows(): lax.all_to_all(summed, 'ep', split_axis=0, concat_axis=0, tiled=True)  25.9 us
    all_to_all x1, starting transfers between devices, serve_rows(): lax.all_to_all(summed, 'ep', split_axis=0, concat_axis=0, tiled=True)  15.3 us
    all_to_all x1, blocking collectives, copy_for_each(): lax.all_to_all(jnp.broadcast_to(array[None], (count, *array.shape)), axis...  7.96 us
    dot_general x2, matrix products, project_rows(): lax.dot_general(row_block, weight, (((1,), (1,)), ((), ())), preferred_el...  6.6 us
  transfers between devices with their start and end apart: 3, of which 3 were waited for; matrix products, arithmetic and copies ran while one was open for 3% of the time, Pallas kernels for 0%

commit v1 on v0

--- a/solution.py
+++ b/solution.py
@@ -5,6 +5,24 @@
 
 TOP = 8
 EXP_DEV = 1
+
+
+def ring_gather(value, axis, dim):
+    ways, here, step = (lax.axis_size(axis), lax.axis_index(axis), value.shape[dim])
+    shape = [n * ways if d == dim else n for d, n in enumerate(value.shape)]
+    full = lax.dynamic_update_slice_in_dim(
+        jnp.zeros(shape, value.dtype), value, here * step, axis=dim
+    )
+    going_up = going_down = value
+    for far in range(1, ways // 2 + 1):
+        going_up = lax.ppermute(going_up, axis, [(d, (d + 1) % ways) for d in range(ways)])
+        full = lax.dynamic_update_slice_in_dim(full, going_up, (here - far) % ways * step, axis=dim)
+        if 2 * far < ways:
+            going_down = lax.ppermute(going_down, axis, [(d, (d - 1) % ways) for d in range(ways)])
+            full = lax.dynamic_update_slice_in_dim(
+                full, going_down, (here + far) % ways * step, axis=dim
+            )
+    return full
 
 
 def copy_for_each(array, axis):
@@ -77,11 +95,8 @@
         experts, hot_most, tokens.shape[1]
     )
     returned_rows, input_peak, hidden_peak = serve_rows(
-        lax.all_gather(
-            lax.all_to_all(outgoing, "ep", split_axis=0, concat_axis=0, tiled=True),
-            "tp",
-            axis=2,
-            tiled=True,
+        ring_gather(
+            lax.all_to_all(outgoing, "ep", split_axis=0, concat_axis=0, tiled=True), "tp", 2
         ),
         gate_weight,
         up_weight,

time: 208 us -> 202 us (0.971)
  waiting for transfers between devices: 96.4 us -> 74.4 us
  starting transfers between devices: 15.4 us -> 29.9 us
  local copies, waits for them, and re-layouts: 7.63 us -> 11.2 us
  matrix products: 9.82 us -> 6.9 us
    all_gather x1 -> x0, waiting for transfers between devices: 33.3 us -> none  [body(): lax.all_gather(lax.all_to_all(outgoing, 'ep', split_axis=0, concat_axis=0...]
    ppermute x0 -> x7, waiting for transfers between devices: none -> 21 us  [the longest x4 21 us: ring_gather(): lax.ppermute(going_up, axis, [(d, (d + 1) % ways) for d in range(ways)])]
    ppermute x0 -> x7, starting transfers between devices: none -> 14.5 us  [the longest x4 14.3 us: ring_gather(): lax.ppermute(going_up, axis, [(d, (d + 1) % ways) for d in range(ways)])]
    reduce_scatter x1, waiting for transfers between devices: 37.1 us -> 27.4 us  [serve_rows(): lax.psum_scatter(partial_value.reshape(senders, slot_count, feat_width).a...]
    dot_general x2, matrix products: 6.6 us -> 3.68 us  [project_rows(): lax.dot_general(row_block, weight, (((1,), (1,)), ((), ())), preferred_el...]
    dynamic_update_slice x0 -> x8, local copies, waits for them, and re-layouts: none -> 2.6 us  [the longest x4 1.3 us: ring_gather(): lax.dynamic_update_slice_in_dim(full, going_up, (here - far) % ways * ste...]
  transfers between devices with their start and end apart: 3 -> 9, of which waited for: 3 -> 6; matrix products, arithmetic and copies ran while one was open for 3% -> 4% of each run, Pallas kernels for 0% -> 0%
where the time goes in v1:
time: 202 us; the launch traced here: 201 us
  waiting for transfers between devices  74.4 us (37%)
  blocking collectives  56.5 us (28%)
  starting transfers between devices  29.9 us (15%)
  between operations  15 us (7%)
  local copies, waits for them, and re-layouts  11.2 us (6%)
  other arithmetic  7.25 us (4%)
  matrix products  6.9 us (3%)
    all_to_all x1, blocking collectives, body(): lax.all_to_all(outgoing, 'ep', split_axis=0, concat_axis=0, tiled=True)  47.6 us
    reduce_scatter x1, waiting for transfers between devices, serve_rows(): lax.psum_scatter(partial_value.reshape(senders, slot_count, feat_width).a...  27.4 us
    all_to_all x1, waiting for transfers between devices, serve_rows(): lax.all_to_all(summed, 'ep', split_axis=0, concat_axis=0, tiled=True)  25.9 us
    ppermute x4, waiting for transfers between devices, ring_gather(): lax.ppermute(going_up, axis, [(d, (d + 1) % ways) for d in range(ways)])  21 us
    all_to_all x1, starting transfers between devices, serve_rows(): lax.all_to_all(summed, 'ep', split_axis=0, concat_axis=0, tiled=True)  15.4 us
    ppermute x4, starting transfers between devices, ring_gather(): lax.ppermute(going_up, axis, [(d, (d + 1) % ways) for d in range(ways)])  14.3 us
    all_to_all x1, blocking collectives, copy_for_each(): lax.all_to_all(jnp.broadcast_to(array[None], (count, *array.shape)), axis...  8.97 us
  transfers between devices with their start and end apart: 9, of which 6 were waited for; matrix products, arithmetic and copies ran while one was open for 4% of the time, Pallas kernels for 0%

profile of v1, /device:TPU:31, one launch (start us, length us, event | category | flops | bytes accessed | tf_op | source)
XLA Modules:
  0.0 201.1 jit_solution(12177182204621807539)
XLA Ops:
  7.2 0.9 copy.21
  8.1 0.7 broadcast_multiply_fusion
  9.5 1.0 scatter_custom_fusion.1
  10.5 1.0 scatter_custom_fusion
  11.6 2.7 %gather_fusion = bf16[512,512]{1,0:T(8,128)(2,1)S(1)} fusion(bf16[16,512]{1,0:T(8,128)(2,1)} %param.6, s32[1024]{0:T(1024)S(1)} %pad_clamp_fusion.1), kind=kCustom, calls=%fused_computation | custom fusion | bytes 1050624 | tf_op jit(solution)/shard_map/gather | solution.py:94
  14.5 47.6 %all_to_all.16 = bf16[64,8,512]{2,1,0:T(8,128)(2,1)S(1)} all-to-all(bf16[64,8,512]{2,1,0:T(8,128)(2,1)S(1)} %bitcast_select_fusion), channel_id=1, replica_groups=mesh['ep'=64,'tp'=8] {'ep'}, dimensions={0} | all-to-all | bytes 1048576 | tf_op jit(solution)/shard_map/all_to_all | solution.py:99
  62.0 3.2 %collective-permute-start = (bf16[64,8,512]{2,1,0:T(8,128)(2,1)S(1)}, bf16[64,8,512]{2,1,0:T(8,128)(2,1)S(1)}, u32[]{:S(2)}, u32[]{:S(2)}) collective-permute-start(bf16[64,8,512]{2,1,0:T(8,128)(2,1)S(1)} %all_to_all.16), channel_id=1, source_target_pairs={{0,1},{1,2},{2,3},{3,4},{4,5},{5,6},{6,7},{7,0},{8,9},{9,10},{10,1... | collective-permute-start | bytes 1572872 | tf_op jit(solution)/shard_map/ppermute | solution.py:18
  65.3 0.2 collective-permute-start.1
  65.4 5.9 %collective-permute-done = bf16[64,8,512]{2,1,0:T(8,128)(2,1)S(1)} collective-permute-done((bf16[64,8,512]{2,1,0:T(8,128)(2,1)S(1)}, bf16[64,8,512]{2,1,0:T(8,128)(2,1)S(1)}, u32[]{:S(2)}, u32[]{:S(2)}) %collective-permute-start) | collective-permute-done | bytes 524320 | tf_op jit(solution)/shard_map/ppermute | solution.py:18
  71.4 3.7 %collective-permute-start.2 = (bf16[64,8,512]{2,1,0:T(8,128)(2,1)S(1)}, bf16[64,8,512]{2,1,0:T(8,128)(2,1)}, u32[]{:S(2)}, u32[]{:S(2)}) collective-permute-start(bf16[64,8,512]{2,1,0:T(8,128)(2,1)S(1)} %collective-permute-done), channel_id=1, source_target_pairs={{0,1},{1,2},{2,3},{3,4},{4,5},{5,6},{6,7},{7,0},{8,9},{9,10},{10,1... | collective-permute-start | bytes 1572872 | tf_op jit(solution)/shard_map/ppermute | solution.py:18
  75.1 6.1 %collective-permute-done.2 = bf16[64,8,512]{2,1,0:T(8,128)(2,1)} collective-permute-done((bf16[64,8,512]{2,1,0:T(8,128)(2,1)S(1)}, bf16[64,8,512]{2,1,0:T(8,128)(2,1)}, u32[]{:S(2)}, u32[]{:S(2)}) %collective-permute-start.2) | collective-permute-done | bytes 524320 | tf_op jit(solution)/shard_map/ppermute | solution.py:18
  81.2 3.8 %collective-permute-start.4 = (bf16[64,8,512]{2,1,0:T(8,128)(2,1)}, bf16[64,8,512]{2,1,0:T(8,128)(2,1)S(1)}, u32[]{:S(2)}, u32[]{:S(2)}) collective-permute-start(bf16[64,8,512]{2,1,0:T(8,128)(2,1)} %collective-permute-done.2), channel_id=1, source_target_pairs={{0,1},{1,2},{2,3},{3,4},{4,5},{5,6},{6,7},{7,0},{8,9},{9,10},{10,1... | collective-permute-start | bytes 1572872 | tf_op jit(solution)/shard_map/ppermute | solution.py:18
  85.0 0.5 broadcast_in_dim.39
  85.6 0.4 copy-done.3
  86.1 5.3 %collective-permute-done.4 = bf16[64,8,512]{2,1,0:T(8,128)(2,1)S(1)} collective-permute-done((bf16[64,8,512]{2,1,0:T(8,128)(2,1)}, bf16[64,8,512]{2,1,0:T(8,128)(2,1)S(1)}, u32[]{:S(2)}, u32[]{:S(2)}) %collective-permute-start.4) | collective-permute-done | bytes 524320 | tf_op jit(solution)/shard_map/ppermute | solution.py:18
  91.4 3.6 %collective-permute-start.6 = (bf16[64,8,512]{2,1,0:T(8,128)(2,1)S(1)}, bf16[64,8,512]{2,1,0:T(8,128)(2,1)S(1)}, u32[]{:S(2)}, u32[]{:S(2)}) collective-permute-start(bf16[64,8,512]{2,1,0:T(8,128)(2,1)S(1)} %collective-permute-done.4), channel_id=1, source_target_pairs={{0,1},{1,2},{2,3},{3,4},{4,5},{5,6},{6,7},{7,0},{8,9},{9,10},{10,1... | collective-permute-start | bytes 1572872 | tf_op jit(solution)/shard_map/ppermute | solution.py:18
  95.1 1.1 constant_dynamic-update-slice_fusion.3
  96.2 1.1 constant_dynamic-update-slice_fusion.2
  97.5 3.6 %collective-permute-done.6 = bf16[64,8,512]{2,1,0:T(8,128)(2,1)S(1)} collective-permute-done((bf16[64,8,512]{2,1,0:T(8,128)(2,1)S(1)}, bf16[64,8,512]{2,1,0:T(8,128)(2,1)S(1)}, u32[]{:S(2)}, u32[]{:S(2)}) %collective-permute-start.6) | collective-permute-done | bytes 524320 | tf_op jit(solution)/shard_map/ppermute | solution.py:18
  101.2 1.5 fusion.2
  102.8 2.1 %abs_reduce_fusion.1 = (bf16[]{:T(256)}, bf16[512,192]{0,1:T(8,128)(2,1)S(1)}) fusion(f32[512,192]{0,1:T(8,128)S(1)} %fusion.2, bf16[1,192,4096]{2,1,0:T(8,128)(2,1)S(1)} %copy-done.6, bf16[64,8,4096]{2,1,0:T(8,128)(2,1)S(1)} %constant_dynamic-update-slice_fusion.7), kind=kOutput, calls=%fused_computation.18 | convolution fusion | flops 806092800 | bytes 6356994 | tf_op jit(solution)/shard_map/dot_general | solution.py:54
  105.1 3.2 %convolution_convert_fusion = bf16[64,8,4096]{2,1,0:T(8,128)(2,1)} fusion(bf16[1,192,4096]{2,1,0:T(8,128)(2,1)S(1)} %copy-done, bf16[512,192]{1,0:T(8,128)(2,1)S(1)} %copy.22), kind=kOutput, calls=%fused_computation.4 | convolution fusion | flops 807403520 | bytes 5963776 | tf_op jit(solution)/shard_map/dot_general | solution.py:65
  108.3 0.7 broadcast_in_dim.46
  109.0 9.0 %all_to_all.17 = f32[8,1,1]{2,1,0:T(1,128)S(1)} all-to-all(f32[8,1,1]{2,1,0:T(1,128)S(1)} %broadcast_in_dim.46), channel_id=1, replica_groups=mesh['ep'=64,'tp'=8] {'tp'}, dimensions={0} | all-to-all | bytes 64 | tf_op jit(solution)/shard_map/all_to_all | solution.py:30
  118.0 27.4 %reduce-scatter.2.cloned.1.call-done = bf16[64,8,512]{2,1,0:T(8,128)(2,1)} async-done(((bf16[64,8,4096]{2,1,0:T(8,128)(2,1)}), bf16[64,8,512]{2,1,0:T(8,128)(2,1)}) %reduce-scatter.2.cloned.1.call-update) | async-done | bytes 524304 | tf_op jit(solution)/shard_map/reduce_scatter | solution.py:66
  145.3 15.4 %all-to-all-start.1 = ((bf16[64,8,512]{2,1,0:T(8,128)(2,1)}), bf16[64,8,512]{2,1,0:T(8,128)(2,1)S(1)}, u32[]{:S(2)}, u32[]{:S(2)}) async-start(bf16[64,8,512]{2,1,0:T(8,128)(2,1)} %reduce-scatter.2.cloned.1.call-done), calls=%async_computation.2 | async-start | bytes 1048576 | tf_op jit(solution)/shard_map/all_to_all | solution.py:72
  160.8 3.4 %abs_reduce_fusion = bf16[]{:T(256)} fusion(bf16[64,8,4096]{2,1,0:T(8,128)(2,1)} %copy-done.1), kind=kLoop, calls=%fused_computation.9 | loop fusion | flops 4194303 | bytes 4194306 | tf_op jit(solution)/shard_map/reduce_max | solution.py:107
  164.8 0.6 reduce_max.46
  165.5 1.2 maximum_bitcast_fusion
  166.7 25.9 %all-to-all-done.1 = bf16[64,8,512]{2,1,0:T(8,128)(2,1)S(1)} async-done(((bf16[64,8,512]{2,1,0:T(8,128)(2,1)}), bf16[64,8,512]{2,1,0:T(8,128)(2,1)S(1)}, u32[]{:S(2)}, u32[]{:S(2)}) %all-to-all-start.1) | async-done | bytes 524320 | tf_op jit(solution)/shard_map/all_to_all | solution.py:72
  192.6 0.8 gather_fusion.1
  193.5 0.8 fusion.7
  (42 shorter events, 1.6 us)
Async XLA Ops:
  7.2 97.9 %copy-start = (bf16[1,192,4096]{2,1,0:T(8,128)(2,1)S(1)}, bf16[1,192,4096]{2,1,0:T(8,128)(2,1)}, u32[]{:S(2)}) copy-start(bf16[1,192,4096]{2,1,0:T(8,128)(2,1)} %param.11) | copy-start | bytes 4718596
  7.2 138.2 %reduce-scatter.2.cloned.1.call-start = ((), (), s32[]{:S(2)}) async-start(), calls=%async_computation.4 | async-start | bytes 4718592 | tf_op jit(solution)/shard_map/reduce_scatter | solution.py:66
  62.0 9.3 %collective-permute-start = (bf16[64,8,512]{2,1,0:T(8,128)(2,1)S(1)}, bf16[64,8,512]{2,1,0:T(8,128)(2,1)S(1)}, u32[]{:S(2)}, u32[]{:S(2)}) collective-permute-start(bf16[64,8,512]{2,1,0:T(8,128)(2,1)S(1)} %all_to_all.16), channel_id=1, source_target_pairs={{0,1},{1,2},{2,3},{3,4},{4,5},{5,6},{6,7},{7,0},{8,9},{9,10},{10,1... | collective-permute-start | bytes 1572872 | tf_op jit(solution)/shard_map/ppermute | solution.py:18
  65.3 9.8 %collective-permute-start.1 = (bf16[64,8,512]{2,1,0:T(8,128)(2,1)S(1)}, bf16[64,8,512]{2,1,0:T(8,128)(2,1)S(1)}, u32[]{:S(2)}, u32[]{:S(2)}) collective-permute-start(bf16[64,8,512]{2,1,0:T(8,128)(2,1)S(1)} %all_to_all.16), channel_id=1, source_target_pairs={{0,7},{1,0},{2,1},{3,2},{4,3},{5,4},{6,5},{7,6},{8,15},{9,8},{10,9... | collective-permute-start | bytes 1572872 | tf_op jit(solution)/shard_map/ppermute | solution.py:21
  71.4 3.7 %copy-start.2 = (bf16[64,8,512]{2,1,0:T(8,128)(2,1)}, bf16[64,8,512]{2,1,0:T(8,128)(2,1)S(1)}, u32[]{:S(2)}) copy-start(bf16[64,8,512]{2,1,0:T(8,128)(2,1)S(1)} %collective-permute-done) | copy-start | bytes 1572868
  71.4 9.8 %collective-permute-start.2 = (bf16[64,8,512]{2,1,0:T(8,128)(2,1)S(1)}, bf16[64,8,512]{2,1,0:T(8,128)(2,1)}, u32[]{:S(2)}, u32[]{:S(2)}) collective-permute-start(bf16[64,8,512]{2,1,0:T(8,128)(2,1)S(1)} %collective-permute-done), channel_id=1, source_target_pairs={{0,1},{1,2},{2,3},{3,4},{4,5},{5,6},{6,7},{7,0},{8,9},{9,10},{10,1... | collective-permute-start | bytes 1572872 | tf_op jit(solution)/shard_map/ppermute | solution.py:18
  75.1 10.5 %collective-permute-start.3 = (bf16[64,8,512]{2,1,0:T(8,128)(2,1)S(1)}, bf16[64,8,512]{2,1,0:T(8,128)(2,1)}, u32[]{:S(2)}, u32[]{:S(2)}) collective-permute-start(bf16[64,8,512]{2,1,0:T(8,128)(2,1)S(1)} %collective-permute-done.1), channel_id=1, source_target_pairs={{0,7},{1,0},{2,1},{3,2},{4,3},{5,4},{6,5},{7,6},{8,15},{9,8},{10,9... | collective-permute-start | bytes 1572872 | tf_op jit(solution)/shard_map/ppermute | solution.py:21
  81.2 10.2 %collective-permute-start.4 = (bf16[64,8,512]{2,1,0:T(8,128)(2,1)}, bf16[64,8,512]{2,1,0:T(8,128)(2,1)S(1)}, u32[]{:S(2)}, u32[]{:S(2)}) collective-permute-start(bf16[64,8,512]{2,1,0:T(8,128)(2,1)} %collective-permute-done.2), channel_id=1, source_target_pairs={{0,1},{1,2},{2,3},{3,4},{4,5},{5,6},{6,7},{7,0},{8,9},{9,10},{10,1... | collective-permute-start | bytes 1572872 | tf_op jit(solution)/shard_map/ppermute | solution.py:18
  85.0 1.0 copy-start.3
  85.5 15.7 %copy-start.5 = (bf16[1,192,4096]{2,1,0:T(8,128)(2,1)S(1)}, bf16[1,192,4096]{2,1,0:T(8,128)(2,1)}, u32[]{:S(2)}) copy-start(bf16[1,192,4096]{2,1,0:T(8,128)(2,1)} %param.9) | copy-start | bytes 4718596
  85.6 11.8 %collective-permute-start.5 = (bf16[64,8,512]{2,1,0:T(8,128)(2,1)}, bf16[64,8,512]{2,1,0:T(8,128)(2,1)S(1)}, u32[]{:S(2)}, u32[]{:S(2)}) collective-permute-start(bf16[64,8,512]{2,1,0:T(8,128)(2,1)} %collective-permute-done.3), channel_id=1, source_target_pairs={{0,7},{1,0},{2,1},{3,2},{4,3},{5,4},{6,5},{7,6},{8,15},{9,8},{10,9... | collective-permute-start | bytes 1572872 | tf_op jit(solution)/shard_map/ppermute | solution.py:21
  91.4 9.7 %collective-permute-start.6 = (bf16[64,8,512]{2,1,0:T(8,128)(2,1)S(1)}, bf16[64,8,512]{2,1,0:T(8,128)(2,1)S(1)}, u32[]{:S(2)}, u32[]{:S(2)}) collective-permute-start(bf16[64,8,512]{2,1,0:T(8,128)(2,1)S(1)} %collective-permute-done.4), channel_id=1, source_target_pairs={{0,1},{1,2},{2,3},{3,4},{4,5},{5,6},{6,7},{7,0},{8,9},{9,10},{10,1... | collective-permute-start | bytes 1572872 | tf_op jit(solution)/shard_map/ppermute | solution.py:18
  97.4 5.4 %copy-start.6 = (bf16[1,192,4096]{2,1,0:T(8,128)(2,1)S(1)}, bf16[1,192,4096]{2,1,0:T(8,128)(2,1)}, u32[]{:S(2)}) copy-start(bf16[1,192,4096]{2,1,0:T(8,128)(2,1)} %param.10) | copy-start | bytes 4718596
  101.2 3.7 %copy-start.1 = (bf16[64,8,4096]{2,1,0:T(8,128)(2,1)}, bf16[64,8,4096]{2,1,0:T(8,128)(2,1)S(1)}, u32[]{:S(2)}) copy-start(bf16[64,8,4096]{2,1,0:T(8,128)(2,1)S(1)} %constant_dynamic-update-slice_fusion.7) | copy-start | bytes 12582916
  105.1 55.6 %copy-start.4 = (f32[16,8]{0,1:T(8,128)S(1)}, f32[16,8]{0,1:T(8,128)}, u32[]{:S(2)}) copy-start(f32[16,8]{0,1:T(8,128)} %param.8) | copy-start | bytes 1540
  145.3 47.3 %all-to-all-start.1 = ((bf16[64,8,512]{2,1,0:T(8,128)(2,1)}), bf16[64,8,512]{2,1,0:T(8,128)(2,1)S(1)}, u32[]{:S(2)}, u32[]{:S(2)}) async-start(bf16[64,8,512]{2,1,0:T(8,128)(2,1)} %reduce-scatter.2.cloned.1.call-done), calls=%async_computation.2 | async-start | bytes 1048576 | tf_op jit(solution)/shard_map/all_to_all | solution.py:72
Sparse Core Ops, SparseCore 0:
  108.5 36.8 reduce-scatter.1
